TPU v7x, 32 devices: a whole 2x2x4 slice. The times are simulated.
32 devices in a mesh: grp: 4 (over y, x), dev: 8 (over z, core).
Axes of the slice: x: 2, y: 2, z: 4, core: 2. Of those that a mesh axis runs over, the one named last changes fastest.
Arguments:
- examples: float32 [2048, 32768], P(('grp', 'dev'))
- labels: int32 [2048], P(('grp', 'dev')), may hold values from 0 to 1, as said below
Outputs:
- consensus: float32 [32768], replicated
- local_weights: float32 [32, 32768], P(('grp', 'dev'))
- dual_vars: float32 [32, 32768], P(('grp', 'dev'))
Inputs may be any that keep to these rules, and one draw needn't show every extreme that they name: `labels`: each example's class, 0 or 1.
All inputs are finite; a program needn't handle non-finite values.
Results may differ from a plain program's by a relative error of at most 0.00012.
Values sent between devices are 32-bit elements; how exact they have to be, the bound alone decides.
A program may use at most 64 MiB of HBM per device.

v0:
```python
import jax
import jax.numpy as jnp
from jax import lax
from jax.sharding import PartitionSpec as P

PROX = 3
ROUNDS = 4


step_size = 200.0
penalty = 0.005
thresh = 0.04


def shrink(values):
    return values - jnp.clip(values, -thresh, thresh)


def local_steps(examples, targets, weight_vector, consensus_point):
    for prox_index in range(PROX):
        label_margins = jnp.dot(examples, weight_vector, precision=lax.Precision.HIGHEST)
        primal_residual = jax.nn.sigmoid(label_margins) - targets
        loss_gradient = jnp.dot(primal_residual, examples, precision=lax.Precision.HIGHEST)
        weight_vector = (
            weight_vector - step_size * loss_gradient + step_size * penalty * consensus_point
        ) / (1.0 + step_size * penalty)
    return weight_vector


def per_device(examples, labels):
    members = lax.axis_size("grp") * lax.axis_size("dev")
    targets = labels.astype(jnp.float32)
    width = examples.shape[1]

    def one_round(round_index, carried):
        consensus, weight_vector, dual_vars = carried
        consensus_point = consensus - dual_vars
        weight_vector = local_steps(examples, targets, weight_vector, consensus_point)
        combined = weight_vector + dual_vars
        summed = lax.psum(combined, ("grp", "dev"))
        consensus = shrink(summed / members)
        dual_vars = dual_vars + weight_vector - consensus
        return (consensus, weight_vector, dual_vars)

    start = (
        jnp.zeros((width,), jnp.float32),
        jnp.zeros((width,), jnp.float32),
        jnp.zeros((width,), jnp.float32),
    )
    consensus, weight_vector, dual_vars = lax.fori_loop(0, ROUNDS, one_round, start)
    return (consensus, weight_vector[None, :], dual_vars[None, :])


def solution(mesh):
    placed = (P(("grp", "dev"), None), P(("grp", "dev")))
    return jax.shard_map(
        per_device,
        mesh=mesh,
        in_specs=placed,
        out_specs=(P(), P(("grp", "dev"), None), P(("grp", "dev"), None)),
        check_vma=False,
    )
```

profile of v0, /device:TPU:0, one launch (start us, length us, event | category | flops | bytes accessed | tf_op | source)
XLA Modules:
  0.0 658.6 jit_solution(14624794344501646285)
XLA Ops:
  7.2 0.7 convert_element_type.3
  7.8 643.4 %while.15 = (s32[]{:T(128)}, f32[32768]{0:T(1024)S(1)}, f32[32768]{0:T(1024)S(1)}, f32[32768]{0:T(1024)S(1)}, f32[64,32768]{1,0:T(8,128)}, /*index=5*/f32[64]{0:T(128)S(1)}, s32[]{:T(128)}, s32[]{:T(128)}) while((s32[]{:T(128)}, f32[32768]{0:T(1024)S(1)}, f32[32768]{0:T(1024)S(1)}, f32[32768]{0:T(1024)S(1)}, ...), condition=%wide.region_2.3_spmd.clone, body=%wide.region_0.2_spmd.clone.sunk | while | flops 151782144 | bytes 88344992 | solution.py:50
  7.9 9.1 %fusion.65 = f32[64,1]{0,1:T(1,128)S(1)} fusion(f32[64]{0:T(128)S(1)} %get-tuple-element.149, f32[64,32768]{1,0:T(8,128)} %get-tuple-element.148, f32[32768,1]{0,1:T(1,128)S(1)} %bitcast.118), kind=kOutput, calls=%fused_computation.20.clone.1 | convolution fusion | flops 25166080 | bytes 8520192 | tf_op jit(solution)/shard_map/while/body/eval_jaxpr/dot_general | solution.py:21
  16.9 4.0 fusion.66
  21.0 6.6 fusion.67
  27.6 4.1 fusion.68
  31.7 6.6 fusion.69
  38.3 4.1 fusion.70
  42.3 0.7 select_add_fusion.2
  43.0 0.0 all-reduce.2.cloned.1.call-update
  43.0 127.3 %all-reduce.2.cloned.1.call-done = f32[32768]{0:T(1024)} async-done(((f32[32768]{0:T(1024)}), f32[32768]{0:T(1024)}) %all-reduce.2.cloned.1.call-update) | async-done | bytes 131088 | tf_op jit(solution)/shard_map/while/body/eval_jaxpr/psum | solution.py:40
  170.4 1.0 fusion.71
  171.4 0.0 all-reduce.2.cloned.1.call-start
  171.5 9.1 %fusion.65 = f32[64,1]{0,1:T(1,128)S(1)} fusion(f32[64]{0:T(128)S(1)} %get-tuple-element.149, f32[64,32768]{1,0:T(8,128)} %get-tuple-element.148, f32[32768,1]{0,1:T(1,128)S(1)} %bitcast.118), kind=kOutput, calls=%fused_computation.20.clone.1 | convolution fusion | flops 25166080 | bytes 8520192 | tf_op jit(solution)/shard_map/while/body/eval_jaxpr/dot_general | solution.py:21
  180.5 4.0 fusion.66
  184.6 6.6 fusion.67
  191.2 4.1 fusion.68
  195.3 6.6 fusion.69
  201.9 4.1 fusion.70
  205.9 0.7 select_add_fusion.2
  206.6 0.0 all-reduce.2.cloned.1.call-update
  206.6 123.7 %all-reduce.2.cloned.1.call-done = f32[32768]{0:T(1024)} async-done(((f32[32768]{0:T(1024)}), f32[32768]{0:T(1024)}) %all-reduce.2.cloned.1.call-update) | async-done | bytes 131088 | tf_op jit(solution)/shard_map/while/body/eval_jaxpr/psum | solution.py:40
  330.3 1.0 fusion.71
  331.3 0.0 all-reduce.2.cloned.1.call-start
  331.4 9.1 %fusion.65 = f32[64,1]{0,1:T(1,128)S(1)} fusion(f32[64]{0:T(128)S(1)} %get-tuple-element.149, f32[64,32768]{1,0:T(8,128)} %get-tuple-element.148, f32[32768,1]{0,1:T(1,128)S(1)} %bitcast.118), kind=kOutput, calls=%fused_computation.20.clone.1 | convolution fusion | flops 25166080 | bytes 8520192 | tf_op jit(solution)/shard_map/while/body/eval_jaxpr/dot_general | solution.py:21
  340.5 4.0 fusion.66
  344.6 6.6 fusion.67
  351.2 4.1 fusion.68
  355.3 6.6 fusion.69
  361.8 4.1 fusion.70
  365.9 0.7 select_add_fusion.2
  366.6 0.0 all-reduce.2.cloned.1.call-update
  366.6 123.7 %all-reduce.2.cloned.1.call-done = f32[32768]{0:T(1024)} async-done(((f32[32768]{0:T(1024)}), f32[32768]{0:T(1024)}) %all-reduce.2.cloned.1.call-update) | async-done | bytes 131088 | tf_op jit(solution)/shard_map/while/body/eval_jaxpr/psum | solution.py:40
  490.3 1.0 fusion.71
  491.3 0.0 all-reduce.2.cloned.1.call-start
  491.4 9.1 %fusion.65 = f32[64,1]{0,1:T(1,128)S(1)} fusion(f32[64]{0:T(128)S(1)} %get-tuple-element.149, f32[64,32768]{1,0:T(8,128)} %get-tuple-element.148, f32[32768,1]{0,1:T(1,128)S(1)} %bitcast.118), kind=kOutput, calls=%fused_computation.20.clone.1 | convolution fusion | flops 25166080 | bytes 8520192 | tf_op jit(solution)/shard_map/while/body/eval_jaxpr/dot_general | solution.py:21
  500.5 4.0 fusion.66
  504.6 6.6 fusion.67
  511.1 4.1 fusion.68
  515.2 6.6 fusion.69
  521.8 4.1 fusion.70
  525.9 0.7 select_add_fusion.2
  526.6 0.0 all-reduce.2.cloned.1.call-update
  526.6 123.7 %all-reduce.2.cloned.1.call-done = f32[32768]{0:T(1024)} async-done(((f32[32768]{0:T(1024)}), f32[32768]{0:T(1024)}) %all-reduce.2.cloned.1.call-update) | async-done | bytes 131088 | tf_op jit(solution)/shard_map/while/body/eval_jaxpr/psum | solution.py:40
  650.3 1.0 fusion.71
  651.3 0.6 copy-done.1
  651.9 0.0 copy-done.2
  652.0 0.0 copy-done.3
  (27 shorter events, 0.4 us)
Async XLA Ops:
  7.8 162.5 %all-reduce.2.cloned.1.call-start = ((), (), s32[]{:S(2)}) async-start(), calls=%async_computation | async-start | bytes 262144 | tf_op jit(solution)/shard_map/while/body/eval_jaxpr/psum | solution.py:40
  7.8 9.1 %copy-start = (f32[64,32768]{1,0:T(8,128)S(1)}, f32[64,32768]{1,0:T(8,128)}, u32[]{:S(2)}) copy-start(f32[64,32768]{1,0:T(8,128)} %get-tuple-element.148) | copy-start | bytes 25165828 | tf_op jit(solution)/shard_map/while
  171.4 159.0 %all-reduce.2.cloned.1.call-start = ((), (), s32[]{:S(2)}) async-start(), calls=%async_computation | async-start | bytes 262144 | tf_op jit(solution)/shard_map/while/body/eval_jaxpr/psum | solution.py:40
  171.4 9.1 %copy-start = (f32[64,32768]{1,0:T(8,128)S(1)}, f32[64,32768]{1,0:T(8,128)}, u32[]{:S(2)}) copy-start(f32[64,32768]{1,0:T(8,128)} %get-tuple-element.148) | copy-start | bytes 25165828 | tf_op jit(solution)/shard_map/while
  331.3 159.0 %all-reduce.2.cloned.1.call-start = ((), (), s32[]{:S(2)}) async-start(), calls=%async_computation | async-start | bytes 262144 | tf_op jit(solution)/shard_map/while/body/eval_jaxpr/psum | solution.py:40
  331.4 9.1 %copy-start = (f32[64,32768]{1,0:T(8,128)S(1)}, f32[64,32768]{1,0:T(8,128)}, u32[]{:S(2)}) copy-start(f32[64,32768]{1,0:T(8,128)} %get-tuple-element.148) | copy-start | bytes 25165828 | tf_op jit(solution)/shard_map/while
  491.3 159.0 %all-reduce.2.cloned.1.call-start = ((), (), s32[]{:S(2)}) async-start(), calls=%async_computation | async-start | bytes 262144 | tf_op jit(solution)/shard_map/while/body/eval_jaxpr/psum | solution.py:40
  491.4 9.1 %copy-start = (f32[64,32768]{1,0:T(8,128)S(1)}, f32[64,32768]{1,0:T(8,128)}, u32[]{:S(2)}) copy-start(f32[64,32768]{1,0:T(8,128)} %get-tuple-element.148) | copy-start | bytes 25165828 | tf_op jit(solution)/shard_map/while
  651.3 0.7 copy-start.1
  651.3 0.7 copy-start.2
  651.3 0.7 copy-start.3
Sparse Core Ops, SparseCore 0:
  43.2 127.1 all-reduce.1
  206.8 123.5 all-reduce.1
  366.7 123.5 all-reduce.1
  526.7 123.5 all-reduce.1
where the time goes:
time: 659 us
  waiting for transfers between devices  498 us (76%)
  matrix products  137 us (21%)
  between operations  13.7 us (2%)
  other arithmetic  7.74 us (1%)
    psum x4, waiting for transfers between devices, one_round(): summed = lax.psum(combined, ('grp', 'dev'))  498 us
    dot_general x12, matrix products, local_steps(): jnp.dot(examples, weight_vector, precision=lax.Precision.HIGHEST)  88.9 us
    dot_general x12, matrix products, local_steps(): jnp.dot(primal_residual, examples, precision=lax.Precision.HIGHEST)  48.6 us
  transfers between devices with their start and end apart: 4, of which 4 were waited for; matrix products, arithmetic and copies ran while one was open for 0% of the time, Pallas kernels for 0%

commit v1 on v0

v1 whole, which is shorter than its diff:
```python
import functools

import jax
import jax.numpy as jnp
from jax import lax
from jax.experimental import pallas as pl
from jax.experimental.pallas import tpu as pltpu
from jax.sharding import PartitionSpec as P

PROX = 3
ROUNDS = 4
step_size = 200.0
penalty = 0.005
thresh = 0.04
shrinkage = 1.0 + step_size * penalty

LANES = 128
SUB = 8
GROUP = LANES * SUB
MESH = pl.DeviceIdType.MESH


def kernel(
    n_grp, n_dev, cores,
    x_hbm, labels_ref,
    z_out, w_out, u_out,
    x, w, u, v, comb, arrived, partial, zfull, gram,
    load_sem, rs_send, rs_recv, line_send, line_recv, ag_send, ag_recv, out_sem,
):
    rows = x.shape[1]
    blocks = x.shape[0]
    plane = n_grp * cores
    line = n_dev // cores
    per = blocks // plane
    members = n_grp * n_dev

    grp = lax.axis_index("grp")
    dev = lax.axis_index("dev")
    core = lax.rem(dev, cores)
    depth = lax.div(dev, cores)
    own = grp * cores + core

    def plane_peer(offset):
        a, b = offset // cores, offset % cores
        other_grp = lax.rem(grp + a, n_grp)
        other_core = lax.rem(core + b, cores)
        return (other_grp, depth * cores + other_core), other_grp * cores + other_core

    def line_peer(offset):
        return (grp, lax.rem(depth + offset, line) * cores + core)

    def load(i):
        return pltpu.make_async_copy(
            x_hbm.at[:, pl.ds(pl.multiple_of(i * GROUP, GROUP), GROUP)], x.at[i], load_sem.at[i]
        )

    def start_load(i, carry):
        load(i).start()
        return carry

    lax.fori_loop(0, blocks, start_load, 0)

    barrier = pltpu.get_barrier_semaphore()
    for offset in range(1, plane):
        pl.semaphore_signal(barrier, inc=1, device_id=plane_peer(offset)[0], device_id_type=MESH)
    for offset in range(1, line):
        pl.semaphore_signal(barrier, inc=1, device_id=line_peer(offset), device_id_type=MESH)

    eye = (
        lax.broadcasted_iota(jnp.int32, (rows, rows), 0) == lax.broadcasted_iota(jnp.int32, (rows, rows), 1)
    ).astype(jnp.float32)
    targets = jnp.sum(eye * labels_ref[...].astype(jnp.float32), axis=1, keepdims=True)

    gram[...] = jnp.zeros_like(gram)
    for ref in (w, u, v):
        ref[...] = jnp.zeros_like(ref)

    def gram_block(i, carry):
        load(i).wait()
        value = x[i]
        high = value.astype(jnp.bfloat16)
        low = (value - high.astype(jnp.float32)).astype(jnp.bfloat16)
        both = jnp.concatenate([high, low], axis=0)
        gram[...] += lax.dot_general(
            both, both, (((1,), (1,)), ((), ())), preferred_element_type=jnp.float32
        )
        return carry

    lax.fori_loop(0, blocks, gram_block, 0)
    full = gram[...]
    g = (full[:rows, :rows] + full[rows:, rows:]) + (full[:rows, rows:] + full[rows:, :rows])

    pl.semaphore_wait(barrier, plane - 1 + line - 1)

    def rs_copy(t, offset):
        device, chunk = plane_peer(offset)
        return pltpu.make_async_remote_copy(
            src_ref=comb.at[pl.ds(chunk * per, per)],
            dst_ref=arrived.at[t, offset - 1],
            send_sem=rs_send.at[t, offset - 1],
            recv_sem=rs_recv.at[t, offset - 1],
            device_id=device,
            device_id_type=MESH,
        )

    def line_copy(t, offset):
        return pltpu.make_async_remote_copy(
            src_ref=partial.at[t, depth],
            dst_ref=partial.at[t, depth],
            send_sem=line_send.at[t, offset - 1],
            recv_sem=line_recv.at[t, offset - 1],
            device_id=line_peer(offset),
            device_id_type=MESH,
        )

    def ag_copy(t, offset):
        device, _ = plane_peer(offset)
        return pltpu.make_async_remote_copy(
            src_ref=zfull.at[t, pl.ds(own * per, per)],
            dst_ref=zfull.at[t, pl.ds(own * per, per)],
            send_sem=ag_send.at[t, offset - 1],
            recv_sem=ag_recv.at[t, offset - 1],
            device_id=device,
            device_id_type=MESH,
        )

    def local_steps(xw, xv):
        total = jnp.zeros_like(xw)
        for prox_index in range(PROX):
            residual = jax.nn.sigmoid(xw) - targets
            across = jnp.sum(eye * residual, axis=0, keepdims=True)
            gr = jnp.sum(g * across, axis=1, keepdims=True)
            xw = (xw - step_size * gr + step_size * penalty * xv) / shrinkage
            total = (total + step_size * residual) / shrinkage
        return xw, total

    w_keep = 1.0 / shrinkage**PROX
    v_gain = step_size * penalty * sum(1.0 / shrinkage ** (k + 1) for k in range(PROX))

    def weights_of(chunk, spread):
        def block(j, carry):
            i = chunk * per + j
            sums = []
            for lane in range(SUB):
                cols = slice(lane * LANES, (lane + 1) * LANES)
                acc = x[i, 0:SUB, cols] * spread[0:SUB]
                for k in range(SUB, rows, SUB):
                    acc += x[i, k : k + SUB, cols] * spread[k : k + SUB]
                sums.append(jnp.sum(acc, axis=0, keepdims=True))
            gradient = jnp.concatenate(sums, axis=0)
            fresh = w_keep * w[i] + v_gain * v[i] - gradient
            w[i] = fresh
            comb[i] = fresh + u[i]
            return carry

        lax.fori_loop(0, per, block, 0)

    def margins_of(t, chunk, accs):
        def block(j, accs):
            i = chunk * per + j
            out = list(accs)
            z = zfull[t, i]
            fresh = comb[i] - z
            u[i] = fresh
            v[i] = z - fresh
            for lane in range(SUB):
                cols = slice(lane * LANES, (lane + 1) * LANES)
                row = jnp.broadcast_to(z[lane : lane + 1], (SUB, LANES))
                for k in range(rows // SUB):
                    out[k] = out[k] + x[i, k * SUB : (k + 1) * SUB, cols] * row
            return tuple(out)

        return lax.fori_loop(0, per, block, accs)

    def duals_of(t, chunk):
        def block(j, carry):
            i = chunk * per + j
            u[i] = comb[i] - zfull[t, i]
            return carry

        lax.fori_loop(0, per, block, 0)

    order = list(range(plane - 1, 0, -1))

    def reduce_round(t, total):
        spread = jnp.broadcast_to(total, (rows, LANES))
        for offset in order:
            weights_of(plane_peer(offset)[1], spread)
            rs_copy(t, offset).start()
        weights_of(own, spread)
        mine = comb[pl.ds(own * per, per)]
        for offset in order[::-1]:
            rs_copy(t, offset).wait_recv()
            mine = mine + arrived[t, offset - 1]
        partial[t, depth] = mine
        for offset in range(1, line):
            line_copy(t, offset).start()
        for offset in range(1, line):
            line_copy(t, offset).wait_recv()
        a = partial[t, 0]
        for k in range(1, line):
            a = a + partial[t, k]
        a = a * (1.0 / members) if members & (members - 1) == 0 else a / members
        zfull[t, pl.ds(own * per, per)] = a - jnp.clip(a, -thresh, thresh)
        for offset in order:
            ag_copy(t, offset).start()

    def sends_done(t):
        for offset in range(1, plane):
            rs_copy(t, offset).wait_send()
            ag_copy(t, offset).wait_send()
        for offset in range(1, line):
            line_copy(t, offset).wait_send()

    def source(offset):
        a, b = offset // cores, offset % cores
        return lax.rem(grp + n_grp - a, n_grp) * cores + lax.rem(core + cores - b, cores)

    def one_round(t, carried):
        xw, xu, xz = carried
        xw, total = local_steps(xw, xz - xu)
        reduce_round(t, total)
        accs = tuple(jnp.zeros((SUB, LANES), jnp.float32) for _ in range(rows // SUB))
        accs = margins_of(t, own, accs)
        for offset in order[::-1]:
            ag_copy(t, offset).wait_recv()
            accs = margins_of(t, source(offset), accs)
        fresh_xz = jnp.sum(jnp.concatenate(accs, axis=0), axis=1, keepdims=True)
        sends_done(t)
        return xw, xu + xw - fresh_xz, fresh_xz

    zero = jnp.zeros((rows, 1), jnp.float32)
    xw, xu, xz = lax.fori_loop(0, ROUNDS - 1, one_round, (zero, zero, zero))

    last = ROUNDS - 1
    _, total = local_steps(xw, xz - xu)
    reduce_round(last, total)
    w_copy = pltpu.make_async_copy(w, w_out, out_sem.at[2 * plane])
    w_copy.start()

    def finish(chunk, slot):
        duals_of(last, chunk)
        span = pl.ds(chunk * per, per)
        copies = (
            pltpu.make_async_copy(zfull.at[last, span], z_out.at[span], out_sem.at[2 * slot]),
            pltpu.make_async_copy(u.at[span], u_out.at[span], out_sem.at[2 * slot + 1]),
        )
        for copy in copies:
            copy.start()
        return copies

    pending = [w_copy, *finish(own, 0)]
    for offset in order[::-1]:
        ag_copy(last, offset).wait_recv()
        pending += finish(source(offset), offset)
    sends_done(last)
    for copy in pending:
        copy.wait()


def per_device(n_grp, n_dev, examples, labels):
    rows, width = examples.shape
    cores = 2 if n_dev % 2 == 0 else 1
    plane, line = n_grp * cores, n_dev // cores
    blocks = width // GROUP
    per = blocks // plane
    vector = jax.ShapeDtypeStruct((blocks, SUB, LANES), jnp.float32)
    anywhere = pl.BlockSpec(memory_space=pltpu.HBM)
    vec = pltpu.VMEM((blocks, SUB, LANES), jnp.float32)
    dma = pltpu.SemaphoreType.DMA
    z, w, u = pl.pallas_call(
        functools.partial(kernel, n_grp, n_dev, cores),
        out_shape=(vector, vector, vector),
        in_specs=[anywhere, pl.BlockSpec(memory_space=pltpu.VMEM)],
        out_specs=(anywhere, anywhere, anywhere),
        scratch_shapes=[
            pltpu.VMEM((blocks, rows, GROUP), jnp.float32),
            vec, vec, vec, vec,
            pltpu.VMEM((ROUNDS, plane - 1, per, SUB, LANES), jnp.float32),
            pltpu.VMEM((ROUNDS, line, per, SUB, LANES), jnp.float32),
            pltpu.VMEM((ROUNDS, blocks, SUB, LANES), jnp.float32),
            pltpu.VMEM((2 * rows, 2 * rows), jnp.float32),
            dma((blocks,)),
            dma((ROUNDS, plane - 1)), dma((ROUNDS, plane - 1)),
            dma((ROUNDS, line - 1)), dma((ROUNDS, line - 1)),
            dma((ROUNDS, plane - 1)), dma((ROUNDS, plane - 1)),
            dma((2 * plane + 1,)),
        ],
        compiler_params=pltpu.CompilerParams(collective_id=0, has_side_effects=True),
    )(examples, labels.reshape(1, rows))
    return z.reshape(width), w.reshape(1, width), u.reshape(1, width)


def solution(mesh):
    placed = (P(("grp", "dev"), None), P(("grp", "dev")))
    return jax.shard_map(
        functools.partial(per_device, mesh.shape["grp"], mesh.shape["dev"]),
        mesh=mesh,
        in_specs=placed,
        out_specs=(P(), P(("grp", "dev"), None), P(("grp", "dev"), None)),
        check_vma=False,
    )
```

time: 659 us -> 68.9 us (0.10)
  waiting for transfers between devices: 498 us -> 0 us
  matrix products: 137 us -> 0 us
  Pallas kernels: 0 us -> 63.4 us
  between operations: 13.7 us -> 0.64 us
  other arithmetic: 7.74 us -> 0 us
    psum x4 -> x0, waiting for transfers between devices: 498 us -> none  [one_round(): summed = lax.psum(combined, ('grp', 'dev'))]
    dot_general x24 -> x0, matrix products: 137 us -> none  [the longest x12 88.9 us: local_steps(): jnp.dot(examples, weight_vector, precision=lax.Precision.HIGHEST)]
    pallas_call x0 -> x1, Pallas kernels: none -> 63.4 us  [per_device(): pl.pallas_call(functools.partial(kernel, n_grp, n_dev, cores), out_shape=...]
  transfers between devices with their start and end apart: 4 -> 0, of which waited for: 4 -> 0; matrix products, arithmetic and copies ran while one was open for 0% -> 0% of each run, Pallas kernels for 0% -> 0%
where the time goes in v1:
time: 68.9 us; the launch traced here: 68.7 us
  Pallas kernels  63.4 us (92%)
  local copies, waits for them, and re-layouts  4.7 us (7%)
    pallas_call x1, Pallas kernels, per_device(): pl.pallas_call(functools.partial(kernel, n_grp, n_dev, cores), out_shape=...  63.4 us
    unnamed x3, local copies, waits for them, and re-layouts  4.7 us

profile of v1, /device:TPU:0, one launch (start us, length us, event | category | flops | bytes accessed | tf_op | source)
XLA Modules:
  0.0 68.7 jit_solution(12568310054416329156)
XLA Ops:
  0.6 63.4 %shard_map.49 = (f32[32,8,128]{2,1,0:T(8,128)}, f32[32,8,128]{2,1,0:T(8,128)}, f32[32,8,128]{2,1,0:T(8,128)}) custom-call(f32[64,32768]{1,0:T(8,128)} %x_hbm.1, s32[1,64]{1,0:T(1,128)} %bitcast.7), custom_call_target="tpu_custom_call" | custom-call | tf_op jit(solution)/shard_map/pallas_call | solution.py:271
  64.0 1.6 %copy.8 = f32[32768]{0:T(1024)} copy(f32[32768]{0:T(1024)} %bitcast.6) | data formatting | bytes 262144
  65.6 1.6 %copy.9 = f32[1,32768]{1,0:T(1,128)} copy(f32[1,32768]{1,0:T(1,128)} %bitcast.5) | data formatting | bytes 262144
  67.1 1.6 %copy.10 = f32[1,32768]{1,0:T(1,128)} copy(f32[1,32768]{1,0:T(1,128)} %bitcast.4) | data formatting | bytes 262144

commit v2 on v1

--- a/solution.py
+++ b/solution.py
@@ -20,11 +20,15 @@
 MESH = pl.DeviceIdType.MESH
 
 
+def shrink(values):
+    return values - jnp.clip(values, -thresh, thresh)
+
+
 def kernel(
     n_grp, n_dev, cores,
     x_hbm, labels_ref,
-    z_out, w_out, u_out,
-    x, w, u, v, comb, arrived, partial, zfull, gram,
+    mean_out, comb_out, u_out,
+    x, w, u, v, comb, arrived, partial, zfull,
     load_sem, rs_send, rs_recv, line_send, line_recv, ag_send, ag_recv, out_sem,
 ):
     rows = x.shape[1]
@@ -71,24 +75,25 @@
     ).astype(jnp.float32)
     targets = jnp.sum(eye * labels_ref[...].astype(jnp.float32), axis=1, keepdims=True)
 
-    gram[...] = jnp.zeros_like(gram)
     for ref in (w, u, v):
         ref[...] = jnp.zeros_like(ref)
 
-    def gram_block(i, carry):
-        load(i).wait()
-        value = x[i]
-        high = value.astype(jnp.bfloat16)
-        low = (value - high.astype(jnp.float32)).astype(jnp.bfloat16)
-        both = jnp.concatenate([high, low], axis=0)
-        gram[...] += lax.dot_general(
-            both, both, (((1,), (1,)), ((), ())), preferred_element_type=jnp.float32
-        )
-        return carry
-
-    lax.fori_loop(0, blocks, gram_block, 0)
-    full = gram[...]
-    g = (full[:rows, :rows] + full[rows:, rows:]) + (full[:rows, rows:] + full[rows:, :rows])
+    def gram_block(step, total):
+        for part in range(batch):
+            i = step * batch + part
+            load(i).wait()
+            value = x[i]
+            high = value.astype(jnp.bfloat16)
+            low = (value - high.astype(jnp.float32)).astype(jnp.bfloat16)
+            total = total + lax.dot_general(
+                jnp.concatenate([high, low], axis=0), high, (((1,), (1,)), ((), ())), preferred_element_type=jnp.float32
+            )
+        return total
+
+    batch = 16
+    pairs = lax.fori_loop(0, blocks // batch, gram_block, jnp.zeros((2 * rows, rows), jnp.float32))
+    mixed = pairs[rows:]
+    g = pairs[:rows] + (mixed + mixed.T)
 
     pl.semaphore_wait(barrier, plane - 1 + line - 1)
 
@@ -172,17 +177,9 @@
 
         return lax.fori_loop(0, per, block, accs)
 
-    def duals_of(t, chunk):
-        def block(j, carry):
-            i = chunk * per + j
-            u[i] = comb[i] - zfull[t, i]
-            return carry
-
-        lax.fori_loop(0, per, block, 0)
-
     order = list(range(plane - 1, 0, -1))
 
-    def reduce_round(t, total):
+    def reduce_round(t, total, point):
         spread = jnp.broadcast_to(total, (rows, LANES))
         for offset in order:
             weights_of(plane_peer(offset)[1], spread)
@@ -201,7 +198,7 @@
         for k in range(1, line):
             a = a + partial[t, k]
         a = a * (1.0 / members) if members & (members - 1) == 0 else a / members
-        zfull[t, pl.ds(own * per, per)] = a - jnp.clip(a, -thresh, thresh)
+        zfull[t, pl.ds(own * per, per)] = point(a)
         for offset in order:
             ag_copy(t, offset).start()
 
@@ -219,7 +216,7 @@
     def one_round(t, carried):
         xw, xu, xz = carried
         xw, total = local_steps(xw, xz - xu)
-        reduce_round(t, total)
+        reduce_round(t, total, shrink)
         accs = tuple(jnp.zeros((SUB, LANES), jnp.float32) for _ in range(rows // SUB))
         accs = margins_of(t, own, accs)
         for offset in order[::-1]:
@@ -234,25 +231,22 @@
 
     last = ROUNDS - 1
     _, total = local_steps(xw, xz - xu)
-    reduce_round(last, total)
-    w_copy = pltpu.make_async_copy(w, w_out, out_sem.at[2 * plane])
-    w_copy.start()
+    u_copy = pltpu.make_async_copy(u, u_out, out_sem.at[plane])
+    u_copy.start()
+    reduce_round(last, total, lambda a: a)
+    comb_copy = pltpu.make_async_copy(comb, comb_out, out_sem.at[plane + 1])
+    comb_copy.start()
 
     def finish(chunk, slot):
-        duals_of(last, chunk)
         span = pl.ds(chunk * per, per)
-        copies = (
-            pltpu.make_async_copy(zfull.at[last, span], z_out.at[span], out_sem.at[2 * slot]),
-            pltpu.make_async_copy(u.at[span], u_out.at[span], out_sem.at[2 * slot + 1]),
-        )
-        for copy in copies:
-            copy.start()
-        return copies
-
-    pending = [w_copy, *finish(own, 0)]
+        copy = pltpu.make_async_copy(zfull.at[last, span], mean_out.at[span], out_sem.at[slot])
+        copy.start()
+        return copy
+
+    pending = [u_copy, comb_copy, finish(own, 0)]
     for offset in order[::-1]:
         ag_copy(last, offset).wait_recv()
-        pending += finish(source(offset), offset)
+        pending.append(finish(source(offset), offset))
     sends_done(last)
     for copy in pending:
         copy.wait()
@@ -268,7 +262,7 @@
     anywhere = pl.BlockSpec(memory_space=pltpu.HBM)
     vec = pltpu.VMEM((blocks, SUB, LANES), jnp.float32)
     dma = pltpu.SemaphoreType.DMA
-    z, w, u = pl.pallas_call(
+    mean, comb, old_u = pl.pallas_call(
         functools.partial(kernel, n_grp, n_dev, cores),
         out_shape=(vector, vector, vector),
         in_specs=[anywhere, pl.BlockSpec(memory_space=pltpu.VMEM)],
@@ -279,16 +273,16 @@
             pltpu.VMEM((ROUNDS, plane - 1, per, SUB, LANES), jnp.float32),
             pltpu.VMEM((ROUNDS, line, per, SUB, LANES), jnp.float32),
             pltpu.VMEM((ROUNDS, blocks, SUB, LANES), jnp.float32),
-            pltpu.VMEM((2 * rows, 2 * rows), jnp.float32),
             dma((blocks,)),
             dma((ROUNDS, plane - 1)), dma((ROUNDS, plane - 1)),
             dma((ROUNDS, line - 1)), dma((ROUNDS, line - 1)),
             dma((ROUNDS, plane - 1)), dma((ROUNDS, plane - 1)),
-            dma((2 * plane + 1,)),
+            dma((plane + 2,)),
         ],
         compiler_params=pltpu.CompilerParams(collective_id=0, has_side_effects=True),
     )(examples, labels.reshape(1, rows))
-    return z.reshape(width), w.reshape(1, width), u.reshape(1, width)
+    z = shrink(mean)
+    return z.reshape(width), (comb - old_u).reshape(1, width), (comb - z).reshape(1, width)
 
 
 def solution(mesh):

time: 68.9 us -> 63.2 us (0.917)
  local copies, waits for them, and re-layouts: 4.7 us -> 0 us
  Pallas kernels: 63.4 us -> 60.6 us
  other arithmetic: 0 us -> 1.79 us
    unnamed x3 -> x0, local copies, waits for them, and re-layouts: 4.7 us -> none
    pallas_call x1, Pallas kernels: 63.4 us -> 60.6 us  [per_device(): pl.pallas_call(functools.partial(kernel, n_grp, n_dev, cores), out_shape=...]
    sub x0 -> x1, other arithmetic: none -> 1.79 us  [per_device(): comb - z]
where the time goes in v2:
time: 63.2 us; the launch traced here: 63 us
  Pallas kernels  60.6 us (96%)
  other arithmetic  1.79 us (3%)
  between operations  0.64 us (1%)
    pallas_call x1, Pallas kernels, per_device(): pl.pallas_call(functools.partial(kernel, n_grp, n_dev, cores), out_shape=...  60.6 us
    sub x1, other arithmetic, per_device(): comb - z  1.79 us

profile of v2, /device:TPU:0, one launch (start us, length us, event | category | flops | bytes accessed | tf_op | source)
XLA Modules:
  0.0 63.0 jit_solution(4889344010779276766)
XLA Ops:
  0.6 60.6 %shard_map.49 = (f32[32,8,128]{2,1,0:T(8,128)}, f32[32,8,128]{2,1,0:T(8,128)}, f32[32,8,128]{2,1,0:T(8,128)}) custom-call(f32[64,32768]{1,0:T(8,128)} %x_hbm.1, s32[1,64]{1,0:T(1,128)} %bitcast.7), custom_call_target="tpu_custom_call" | custom-call | tf_op jit(solution)/shard_map/pallas_call | solution.py:265
  61.2 1.8 %fusion = (f32[32,8,128]{2,1,0:T(8,128)}, f32[32768]{0:T(1024)}, f32[32,8,128]{2,1,0:T(8,128)}) fusion(f32[32,8,128]{2,1,0:T(8,128)} %get-tuple-element.7, f32[32,8,128]{2,1,0:T(8,128)} %get-tuple-element.6, f32[32,8,128]{2,1,0:T(8,128)} %get-tuple-element.8), kind=kLoop, calls=%fused_computation.1 | loop fusion | flops 131072 | bytes 786432 | tf_op jit(solution)/shard_map/sub | solution.py:285

commit v3 on v2

v3 whole, which is shorter than its diff:
```python
import functools

import jax
import jax.numpy as jnp
from jax import lax
from jax.experimental import pallas as pl
from jax.experimental.pallas import tpu as pltpu
from jax.sharding import PartitionSpec as P

PROX = 3
PARTS = 2
ROUNDS = 4
step_size = 200.0
penalty = 0.005
thresh = 0.04
shrinkage = 1.0 + step_size * penalty

LANES = 128
SUB = 8
GROUP = LANES * SUB
MESH = pl.DeviceIdType.MESH


def shrink(values):
    return values - jnp.clip(values, -thresh, thresh)


def kernel(
    n_grp, n_dev, cores, parts,
    x_hbm, labels_ref,
    mean_out, comb_out, u_out,
    x, w, u, v, comb, arrived, partial, zfull,
    load_sem, rs_send, rs_recv, line_send, line_recv, ag_send, ag_recv, out_sem,
):
    rows = x.shape[1]
    blocks = x.shape[0]
    plane = n_grp * cores
    line = n_dev // cores
    per = blocks // plane
    piece = per // parts
    members = n_grp * n_dev

    grp = lax.axis_index("grp")
    dev = lax.axis_index("dev")
    core = lax.rem(dev, cores)
    depth = lax.div(dev, cores)
    own = grp * cores + core

    def shift(position, size, offset):
        if size % 2:
            return lax.rem(position + (offset + size) % size, size)
        half = size // 2
        high = lax.rem(lax.div(position, 2) + (offset // 2 if offset > 0 else half - (-offset) // 2), half)
        return high * 2 + lax.rem(position + abs(offset) % 2, 2)

    def plane_member(offset, sign):
        return shift(grp, n_grp, sign * (offset // cores)), lax.rem(core + offset % cores, cores)

    def plane_peer(offset):
        other_grp, other_core = plane_member(offset, 1)
        return (other_grp, depth * cores + other_core), other_grp * cores + other_core

    def source(offset):
        other_grp, other_core = plane_member(offset, -1)
        return other_grp * cores + other_core

    def line_peer(offset):
        return (grp, shift(depth, line, offset) * cores + core)

    def load(i):
        return pltpu.make_async_copy(
            x_hbm.at[:, pl.ds(pl.multiple_of(i * GROUP, GROUP), GROUP)], x.at[i], load_sem.at[i]
        )

    def start_load(i, carry):
        load(i).start()
        return carry

    lax.fori_loop(0, blocks, start_load, 0)

    barrier = pltpu.get_barrier_semaphore()
    for offset in range(1, plane):
        pl.semaphore_signal(barrier, inc=1, device_id=plane_peer(offset)[0], device_id_type=MESH)
    for offset in range(1, line):
        pl.semaphore_signal(barrier, inc=1, device_id=line_peer(offset), device_id_type=MESH)

    eye = (
        lax.broadcasted_iota(jnp.int32, (rows, rows), 0) == lax.broadcasted_iota(jnp.int32, (rows, rows), 1)
    ).astype(jnp.float32)
    across = labels_ref[...].astype(jnp.float32)
    targets = jnp.sum(eye * across, axis=1, keepdims=True), across

    for ref in (w, u, v):
        ref[...] = jnp.zeros_like(ref)

    def gram_block(step, total):
        for part in range(batch):
            i = step * batch + part
            load(i).wait()
            value = x[i]
            high = value.astype(jnp.bfloat16)
            low = (value - high.astype(jnp.float32)).astype(jnp.bfloat16)
            total = total + lax.dot_general(
                jnp.concatenate([high, low], axis=0), high, (((1,), (1,)), ((), ())), preferred_element_type=jnp.float32
            )
        return total

    batch = 16
    pairs = lax.fori_loop(0, blocks // batch, gram_block, jnp.zeros((2 * rows, rows), jnp.float32))
    mixed = pairs[rows:]
    g = pairs[:rows] + (mixed + mixed.T)

    pl.semaphore_wait(barrier, plane - 1 + line - 1)

    def rs_copy(t, h, offset):
        device, chunk = plane_peer(offset)
        return pltpu.make_async_remote_copy(
            src_ref=comb.at[pl.ds(chunk * per + h * piece, piece)],
            dst_ref=arrived.at[t, h, offset - 1],
            send_sem=rs_send.at[t, h, offset - 1],
            recv_sem=rs_recv.at[t, h, offset - 1],
            device_id=device,
            device_id_type=MESH,
        )

    def line_copy(t, h, offset):
        return pltpu.make_async_remote_copy(
            src_ref=partial.at[t, h, depth],
            dst_ref=partial.at[t, h, depth],
            send_sem=line_send.at[t, h, offset - 1],
            recv_sem=line_recv.at[t, h, offset - 1],
            device_id=line_peer(offset),
            device_id_type=MESH,
        )

    def ag_copy(t, h, offset):
        device, _ = plane_peer(offset)
        span = pl.ds(own * per + h * piece, piece)
        return pltpu.make_async_remote_copy(
            src_ref=zfull.at[t, span],
            dst_ref=zfull.at[t, span],
            send_sem=ag_send.at[t, h, offset - 1],
            recv_sem=ag_recv.at[t, h, offset - 1],
            device_id=device,
            device_id_type=MESH,
        )

    def turned(value, axis):
        return jnp.sum(eye * value, axis=axis, keepdims=True)

    def local_steps(xw, xv):
        total = jnp.zeros_like(xw)
        both_xv = xv, turned(xv, 0)
        for prox_index in range(PROX - 1):
            axis = prox_index % 2
            residual = jax.nn.sigmoid(xw) - targets[axis]
            moved = jnp.sum(eye * xw - step_size * (g * residual), axis=axis, keepdims=True)
            xw = (moved + step_size * penalty * both_xv[1 - axis]) / shrinkage
            total = (total + step_size * (turned(residual, 1) if axis else residual)) / shrinkage
        if PROX % 2 == 0:
            xw = turned(xw, 1)
        residual = jax.nn.sigmoid(xw) - targets[0]
        total = (total + step_size * residual) / shrinkage

        def finish_step():
            moved = jnp.sum(g * turned(residual, 0), axis=1, keepdims=True)
            return (xw - step_size * moved + step_size * penalty * xv) / shrinkage

        return finish_step, total

    w_keep = 1.0 / shrinkage**PROX
    v_gain = step_size * penalty * sum(1.0 / shrinkage ** (k + 1) for k in range(PROX))

    def weights_of(chunk, h, spread):
        def block(j, carry):
            i = chunk * per + h * piece + j
            sums = []
            for lane in range(SUB):
                cols = slice(lane * LANES, (lane + 1) * LANES)
                acc = x[i, 0:SUB, cols] * spread[0:SUB]
                for k in range(SUB, rows, SUB):
                    acc += x[i, k : k + SUB, cols] * spread[k : k + SUB]
                sums.append(jnp.sum(acc, axis=0, keepdims=True))
            gradient = jnp.concatenate(sums, axis=0)
            fresh = w_keep * w[i] + v_gain * v[i] - gradient
            w[i] = fresh
            comb[i] = fresh + u[i]
            return carry

        lax.fori_loop(0, piece, block, 0)

    def margins_of(t, chunk, h, accs):
        def block(j, accs):
            i = chunk * per + h * piece + j
            out = list(accs)
            z = zfull[t, i]
            fresh = comb[i] - z
            u[i] = fresh
            v[i] = z - fresh
            for lane in range(SUB):
                cols = slice(lane * LANES, (lane + 1) * LANES)
                row = jnp.broadcast_to(z[lane : lane + 1], (SUB, LANES))
                for k in range(rows // SUB):
                    out[k] = out[k] + x[i, k * SUB : (k + 1) * SUB, cols] * row
            return tuple(out)

        return lax.fori_loop(0, piece, block, accs)

    order = list(range(plane - 1, 0, -1))

    def reduce_round(t, total, point):
        spread = jnp.broadcast_to(total, (rows, LANES))
        for h in range(parts):
            for offset in order:
                weights_of(plane_peer(offset)[1], h, spread)
                rs_copy(t, h, offset).start()
        for h in range(parts):
            weights_of(own, h, spread)
        for h in range(parts):
            mine = comb[pl.ds(own * per + h * piece, piece)]
            for offset in order[::-1]:
                rs_copy(t, h, offset).wait_recv()
                mine = mine + arrived[t, h, offset - 1]
            partial[t, h, depth] = mine
            for offset in range(line - 1, 0, -1):
                line_copy(t, h, offset).start()
        for h in range(parts):
            for offset in range(1, line):
                line_copy(t, h, offset).wait_recv()
            a = partial[t, h, 0]
            for k in range(1, line):
                a = a + partial[t, h, k]
            a = a * (1.0 / members) if members & (members - 1) == 0 else a / members
            zfull[t, pl.ds(own * per + h * piece, piece)] = point(a)
            for offset in order:
                ag_copy(t, h, offset).start()

    def sends_done(t):
        for h in range(parts):
            for offset in range(1, plane):
                rs_copy(t, h, offset).wait_send()
                ag_copy(t, h, offset).wait_send()
            for offset in range(1, line):
                line_copy(t, h, offset).wait_send()

    def one_round(t, carried):
        xw, xu, xz = carried
        finish_step, total = local_steps(xw, xz - xu)
        reduce_round(t, total, shrink)
        xw = finish_step()
        accs = tuple(jnp.zeros((SUB, LANES), jnp.float32) for _ in range(rows // SUB))
        for h in range(parts):
            accs = margins_of(t, own, h, accs)
        for h in range(parts):
            for offset in order[::-1]:
                ag_copy(t, h, offset).wait_recv()
                accs = margins_of(t, source(offset), h, accs)
        fresh_xz = jnp.sum(jnp.concatenate(accs, axis=0), axis=1, keepdims=True)
        sends_done(t)
        return xw, xu + xw - fresh_xz, fresh_xz

    zero = jnp.zeros((rows, 1), jnp.float32)
    xw, xu, xz = lax.fori_loop(0, ROUNDS - 1, one_round, (zero, zero, zero))

    last = ROUNDS - 1
    _, total = local_steps(xw, xz - xu)
    u_copy = pltpu.make_async_copy(u, u_out, out_sem.at[plane])
    u_copy.start()
    reduce_round(last, total, lambda a: a)
    comb_copy = pltpu.make_async_copy(comb, comb_out, out_sem.at[plane + 1])
    comb_copy.start()

    def finish(chunk, slot):
        span = pl.ds(chunk * per, per)
        copy = pltpu.make_async_copy(zfull.at[last, span], mean_out.at[span], out_sem.at[slot])
        copy.start()
        return copy

    pending = [u_copy, comb_copy, finish(own, 0)]
    for offset in order[::-1]:
        for h in range(parts):
            ag_copy(last, h, offset).wait_recv()
        pending.append(finish(source(offset), offset))
    sends_done(last)
    for copy in pending:
        copy.wait()


def per_device(n_grp, n_dev, examples, labels):
    rows, width = examples.shape
    cores = 2 if n_dev % 2 == 0 else 1
    plane, line = n_grp * cores, n_dev // cores
    blocks = width // GROUP
    per = blocks // plane
    parts = PARTS if per % PARTS == 0 else 1
    vector = jax.ShapeDtypeStruct((blocks, SUB, LANES), jnp.float32)
    anywhere = pl.BlockSpec(memory_space=pltpu.HBM)
    vec = pltpu.VMEM((blocks, SUB, LANES), jnp.float32)
    dma = pltpu.SemaphoreType.DMA
    mean, comb, old_u = pl.pallas_call(
        functools.partial(kernel, n_grp, n_dev, cores, parts),
        out_shape=(vector, vector, vector),
        in_specs=[anywhere, pl.BlockSpec(memory_space=pltpu.VMEM)],
        out_specs=(anywhere, anywhere, anywhere),
        scratch_shapes=[
            pltpu.VMEM((blocks, rows, GROUP), jnp.float32),
            vec, vec, vec, vec,
            pltpu.VMEM((ROUNDS, parts, plane - 1, per // parts, SUB, LANES), jnp.float32),
            pltpu.VMEM((ROUNDS, parts, line, per // parts, SUB, LANES), jnp.float32),
            pltpu.VMEM((ROUNDS, blocks, SUB, LANES), jnp.float32),
            dma((blocks,)),
            dma((ROUNDS, parts, plane - 1)), dma((ROUNDS, parts, plane - 1)),
            dma((ROUNDS, parts, line - 1)), dma((ROUNDS, parts, line - 1)),
            dma((ROUNDS, parts, plane - 1)), dma((ROUNDS, parts, plane - 1)),
            dma((plane + 2,)),
        ],
        compiler_params=pltpu.CompilerParams(collective_id=0, has_side_effects=True),
    )(examples, labels.reshape(1, rows))
    z = shrink(mean)
    return z.reshape(width), (comb - old_u).reshape(1, width), (comb - z).reshape(1, width)


def solution(mesh):
    placed = (P(("grp", "dev"), None), P(("grp", "dev")))
    return jax.shard_map(
        functools.partial(per_device, mesh.shape["grp"], mesh.shape["dev"]),
        mesh=mesh,
        in_specs=placed,
        out_specs=(P(), P(("grp", "dev"), None), P(("grp", "dev"), None)),
        check_vma=False,
    )
```

time: 63.2 us -> 59.8 us (0.946)
  Pallas kernels: 60.6 us -> 57.2 us
    pallas_call x1, Pallas kernels: 60.6 us -> 57.2 us  [per_device(): pl.pallas_call(functools.partial(kernel, n_grp, n_dev, cores, parts), out...]
where the time goes in v3:
time: 59.8 us; the launch traced here: 59.7 us
  Pallas kernels  57.2 us (96%)
  other arithmetic  1.79 us (3%)
  between operations  0.64 us (1%)
    pallas_call x1, Pallas kernels, per_device(): pl.pallas_call(functools.partial(kernel, n_grp, n_dev, cores, parts), out...  57.2 us
    sub x1, other arithmetic, per_device(): comb - z  1.79 us

profile of v3, /device:TPU:0, one launch (start us, length us, event | category | flops | bytes accessed | tf_op | source)
XLA Modules:
  0.0 59.7 jit_solution(18212344011850816582)
XLA Ops:
  0.6 57.2 %shard_map.49 = (f32[32,8,128]{2,1,0:T(8,128)}, f32[32,8,128]{2,1,0:T(8,128)}, f32[32,8,128]{2,1,0:T(8,128)}) custom-call(f32[64,32768]{1,0:T(8,128)} %x_hbm.1, s32[1,64]{1,0:T(1,128)} %bitcast.7), custom_call_target="tpu_custom_call" | custom-call | tf_op jit(solution)/shard_map/pallas_call | solution.py:300
  57.9 1.8 %fusion = (f32[32,8,128]{2,1,0:T(8,128)}, f32[32768]{0:T(1024)}, f32[32,8,128]{2,1,0:T(8,128)}) fusion(f32[32,8,128]{2,1,0:T(8,128)} %get-tuple-element.7, f32[32,8,128]{2,1,0:T(8,128)} %get-tuple-element.6, f32[32,8,128]{2,1,0:T(8,128)} %get-tuple-element.8), kind=kLoop, calls=%fused_computation.1 | loop fusion | flops 131072 | bytes 786432 | tf_op jit(solution)/shard_map/sub | solution.py:320

commit v4 on v3

--- a/solution.py
+++ b/solution.py
@@ -187,7 +187,7 @@
             comb[i] = fresh + u[i]
             return carry
 
-        lax.fori_loop(0, piece, block, 0)
+        lax.fori_loop(0, piece, block, 0, unroll=True)
 
     def margins_of(t, chunk, h, accs):
         def block(j, accs):
@@ -204,7 +204,7 @@
                     out[k] = out[k] + x[i, k * SUB : (k + 1) * SUB, cols] * row
             return tuple(out)
 
-        return lax.fori_loop(0, piece, block, accs)
+        return lax.fori_loop(0, piece, block, accs, unroll=True)
 
     order = list(range(plane - 1, 0, -1))
 

time: 59.8 us -> 59.1 us (0.988)
  Pallas kernels: 57.2 us -> 56.5 us
    pallas_call x1, Pallas kernels: 57.2 us -> 56.5 us  [per_device(): pl.pallas_call(functools.partial(kernel, n_grp, n_dev, cores, parts), out...]
where the time goes in v4:
time: 59.1 us; the launch traced here: 58.9 us
  Pallas kernels  56.5 us (96%)
  other arithmetic  1.79 us (3%)
  between operations  0.64 us (1%)
    pallas_call x1, Pallas kernels, per_device(): pl.pallas_call(functools.partial(kernel, n_grp, n_dev, cores, parts), out...  56.5 us
    sub x1, other arithmetic, per_device(): comb - z  1.79 us

profile of v4, /device:TPU:0, one launch (start us, length us, event | category | flops | bytes accessed | tf_op | source)
XLA Modules:
  0.0 58.9 jit_solution(5769784708482394410)
XLA Ops:
  0.6 56.5 %shard_map.49 = (f32[32,8,128]{2,1,0:T(8,128)}, f32[32,8,128]{2,1,0:T(8,128)}, f32[32,8,128]{2,1,0:T(8,128)}) custom-call(f32[64,32768]{1,0:T(8,128)} %x_hbm.1, s32[1,64]{1,0:T(1,128)} %bitcast.7), custom_call_target="tpu_custom_call" | custom-call | tf_op jit(solution)/shard_map/pallas_call | solution.py:300
  57.1 1.8 %fusion = (f32[32,8,128]{2,1,0:T(8,128)}, f32[32768]{0:T(1024)}, f32[32,8,128]{2,1,0:T(8,128)}) fusion(f32[32,8,128]{2,1,0:T(8,128)} %get-tuple-element.7, f32[32,8,128]{2,1,0:T(8,128)} %get-tuple-element.6, f32[32,8,128]{2,1,0:T(8,128)} %get-tuple-element.8), kind=kLoop, calls=%fused_computation.1 | loop fusion | flops 131072 | bytes 786432 | tf_op jit(solution)/shard_map/sub | solution.py:320

commit v5 on v4

--- a/solution.py
+++ b/solution.py
@@ -94,10 +94,11 @@
         ref[...] = jnp.zeros_like(ref)
 
     def gram_block(step, total):
-        for part in range(batch):
-            i = step * batch + part
+        for part in range(batch // 2):
+            i = step * batch + part * 2
             load(i).wait()
-            value = x[i]
+            load(i + 1).wait()
+            value = jnp.concatenate([x[i], x[i + 1]], axis=1)
             high = value.astype(jnp.bfloat16)
             low = (value - high.astype(jnp.float32)).astype(jnp.bfloat16)
             total = total + lax.dot_general(
@@ -216,7 +217,6 @@
                 rs_copy(t, h, offset).start()
         for h in range(parts):
             weights_of(own, h, spread)
-        for h in range(parts):
             mine = comb[pl.ds(own * per + h * piece, piece)]
             for offset in order[::-1]:
                 rs_copy(t, h, offset).wait_recv()

time: 59.1 us -> 58.9 us (level)
  no operation moved by 1% of the time
where the time goes in v5:
time: 58.9 us; the launch traced here: 58.7 us
  Pallas kernels  56.3 us (96%)
  other arithmetic  1.79 us (3%)
  between operations  0.64 us (1%)
    pallas_call x1, Pallas kernels, per_device(): pl.pallas_call(functools.partial(kernel, n_grp, n_dev, cores, parts), out...  56.3 us
    sub x1, other arithmetic, per_device(): comb - z  1.79 us

profile of v5, /device:TPU:0, one launch (start us, length us, event | category | flops | bytes accessed | tf_op | source)
XLA Modules:
  0.0 58.7 jit_solution(932618335831987290)
XLA Ops:
  0.6 56.3 %shard_map.49 = (f32[32,8,128]{2,1,0:T(8,128)}, f32[32,8,128]{2,1,0:T(8,128)}, f32[32,8,128]{2,1,0:T(8,128)}) custom-call(f32[64,32768]{1,0:T(8,128)} %x_hbm.1, s32[1,64]{1,0:T(1,128)} %bitcast.7), custom_call_target="tpu_custom_call" | custom-call | tf_op jit(solution)/shard_map/pallas_call | solution.py:300
  56.9 1.8 %fusion = (f32[32,8,128]{2,1,0:T(8,128)}, f32[32768]{0:T(1024)}, f32[32,8,128]{2,1,0:T(8,128)}) fusion(f32[32,8,128]{2,1,0:T(8,128)} %get-tuple-element.7, f32[32,8,128]{2,1,0:T(8,128)} %get-tuple-element.6, f32[32,8,128]{2,1,0:T(8,128)} %get-tuple-element.8), kind=kLoop, calls=%fused_computation.1 | loop fusion | flops 131072 | bytes 786432 | tf_op jit(solution)/shard_map/sub | solution.py:320
